TPU v7x, 32 devices: a whole 2x2x4 slice. The times are simulated.
32 devices in a mesh: cluster: 4 (over x, core), leaf: 8 (over z, y).
Axes of the slice: x: 2, y: 2, z: 4, core: 2. Of those that a mesh axis runs over, the one named last changes fastest.
Arguments:
- probes: float32 [32768, 512], P(('cluster', 'leaf')), may hold values from -6 to 6
- dense_leaf: float32 [32768, 1024], P(('cluster', 'leaf')), may hold values from -0.1875 to 0.1875
- leaf_basis: float32 [32768, 128], P(('cluster', 'leaf')), may hold values from -0.1875 to 0.1875
- sibling_cores: float32 [32, 8, 128, 128], P(('cluster', 'leaf')), may hold values from -0.5 to 0.5
- transfer: float32 [32, 128, 128], P(('cluster', 'leaf')), may hold values from -0.5 to 0.5
- cluster_cores: float32 [4, 4, 128, 128], P('cluster'), may hold values from -0.1875 to 0.1875
Outputs:
- product: float32 [32768, 512], P(('cluster', 'leaf'))
All inputs are finite; a program needn't handle non-finite values.
Results may differ from a plain program's by a relative error of at most 0.00005.
Values sent between devices are 32-bit elements; how exact they have to be, the bound alone decides.
No kernel may reach another device: no remote copies, remote signals or barrier semaphores. Data moves between devices by JAX's collectives and lax.ppermute only.
A program may use at most 128 MiB of HBM per device.

v0:
```python
import jax
import jax.numpy as jnp
from jax import lax
from jax.sharding import PartitionSpec as P

HI = lax.Precision.HIGHEST


def local(probes, dense_leaf, leaf_basis, sibling_cores, transfer, cluster_cores):
    own = lax.axis_index("leaf")
    cown = lax.axis_index("cluster")
    cores = sibling_cores[0]
    trans = transfer[0]
    outer_cores = cluster_cores[0]
    rank_two = trans.shape[1]
    near = jnp.dot(dense_leaf, probes, precision=HI) + jnp.dot(dense_leaf.T, probes, precision=HI)
    coef = jnp.dot(leaf_basis.T, probes, precision=HI)
    turned = lax.all_to_all(cores, "leaf", split_axis=0, concat_axis=0, tiled=True)
    used = cores + jnp.transpose(turned, (0, 2, 1))
    piece = lax.all_gather(coef[None], "leaf", axis=0, tiled=True)
    count = piece.shape[0]
    block = used
    keep = (jnp.arange(count, dtype=jnp.int32) != own).astype(jnp.float32)
    block = block * keep[:, None, None]
    sib = jnp.einsum("jab,jbp->ap", block, piece, precision=HI)
    local_g = jnp.dot(trans.T, coef, precision=HI)
    nclu = outer_cores.shape[0]
    bkeep = (jnp.arange(nclu, dtype=jnp.int32) != cown).astype(jnp.float32)[:, None, None]
    masked = outer_cores * bkeep
    g_whole = lax.psum(local_g, "leaf")
    gathered = lax.all_gather(g_whole[None], "cluster", axis=0, tiled=True)
    front = jnp.einsum("dab,dbp->ap", masked, gathered, precision=HI)
    number = rank_two * lax.axis_size("cluster") // rank_two
    block = masked
    terms = jnp.einsum("dba,bp->dap", block, g_whole, precision=HI)
    field = front + lax.psum_scatter(
        terms.reshape(number * rank_two, g_whole.shape[1]),
        "cluster",
        scatter_dimension=0,
        tiled=True,
    )
    total = sib + jnp.dot(trans, field, precision=HI)
    return near + jnp.dot(leaf_basis, total, precision=HI)


def solution(mesh):
    return jax.shard_map(
        local,
        mesh=mesh,
        in_specs=(
            P(("cluster", "leaf"), None),
            P(("cluster", "leaf"), None),
            P(("cluster", "leaf"), None),
            P(("cluster", "leaf"), None, None, None),
            P(("cluster", "leaf"), None, None),
            P("cluster", None, None, None),
        ),
        out_specs=P(("cluster", "leaf"), None),
        check_vma=False,
    )
```

profile of v0, /device:TPU:0, one launch (start us, length us, event | category | flops | bytes accessed | tf_op | source)
XLA Modules:
  0.0 197.5 jit_solution(9313554170039844846)
XLA Ops:
  6.5 0.0 copy-start
  6.5 0.0 copy-start.6
  6.5 0.0 copy-start.5
  6.5 0.0 all-reduce.2.cloned.1.call-start
  6.5 1.6 copy-done
  8.1 2.4 %fusion.10 = f32[128,512]{1,0:T(8,128)S(1)} fusion(f32[1024,128]{1,0:T(8,128)} %param.8, f32[1024,512]{1,0:T(8,128)S(1)} %copy-done), kind=kOutput, calls=%fused_computation.18 | convolution fusion | flops 805306368 | bytes 2883584 | tf_op jit(solution)/shard_map/dot_general | solution.py:17
  10.5 0.0 copy-start.3
  10.6 0.0 copy-done.6
  10.6 1.3 convolution_bitcast_fusion.3
  11.9 0.0 all-reduce.2.cloned.1.call-update
  11.9 0.0 all-gather.7.cloned.1.call-start
  11.9 73.8 %all-reduce.2.cloned.1.call-done = f32[128,512]{0,1:T(8,128)} async-done(((f32[128,512]{0,1:T(8,128)}), f32[128,512]{0,1:T(8,128)}) %all-reduce.2.cloned.1.call-update) | async-done | bytes 262160 | tf_op jit(solution)/shard_map/psum | solution.py:30
  85.8 0.0 copy-start.4
  85.8 0.0 all-gather.7.cloned.1.call-update
  85.8 0.0 reduce-scatter.2.cloned.1.call-start
  85.8 0.0 copy-done.5
  85.8 0.1 copy.10
  86.0 0.1 bitcast_multiply_fusion
  86.1 2.9 %fusion.11 = f32[512,512]{1,0:T(8,128)} fusion(f32[512,128]{1,0:T(8,128)S(1)} %bitcast.52, f32[128,512]{0,1:T(8,128)} %all-reduce.2.cloned.1.call-done), kind=kOutput, calls=%fused_computation.19 | convolution fusion | flops 402653184 | bytes 1572864 | tf_op jit(solution)/shard_map/dba,bp->dap/dot_general | solution.py:35
  89.0 0.0 reduce-scatter.2.cloned.1.call-update
  89.0 0.0 copy-done.3
  89.1 0.0 all-gather.5.cloned.1.call-start
  89.1 0.5 all-gather.5.cloned.1.call-update
  89.6 0.0 copy-done.4
  89.6 1.0 copy.9
  90.6 4.3 %all-to-all-start = ((f32[8,128,128]{1,2,0:T(8,128)}), f32[8,128,128]{1,2,0:T(8,128)}, u32[]{:S(2)}, u32[]{:S(2)}) async-start(f32[8,128,128]{1,2,0:T(8,128)} %copy.9), calls=%async_computation | async-start | bytes 1048576 | tf_op jit(solution)/shard_map/all_to_all | solution.py:18
  95.0 9.6 %fusion.8 = f32[1024,512]{1,0:T(8,128)} fusion(f32[1024,1024]{1,0:T(8,128)} %param.7, f32[1024,512]{1,0:T(8,128)S(1)} %copy-done), kind=kOutput, calls=%fused_computation.16 | convolution fusion | flops 6442450944 | bytes 8388608 | tf_op jit(solution)/shard_map/dot_general | solution.py:16
  104.6 9.6 %fusion.9 = f32[1024,512]{1,0:T(8,128)} fusion(f32[1024,1024]{1,0:T(8,128)} %param.7, f32[1024,512]{1,0:T(8,128)S(1)} %copy-done), kind=kOutput, calls=%fused_computation.17 | convolution fusion | flops 6442450944 | bytes 8388608 | tf_op jit(solution)/shard_map/dot_general | solution.py:16
  114.2 0.0 all-gather.7.cloned.1.call-done
  114.2 1.6 copy.14
  115.8 15.0 %reduce-scatter.2.cloned.1.call-done = f32[128,512]{1,0:T(8,128)} async-done(((f32[512,512]{1,0:T(8,128)}), f32[128,512]{1,0:T(8,128)}) %reduce-scatter.2.cloned.1.call-update) | async-done | bytes 262160 | tf_op jit(solution)/shard_map/reduce_scatter | solution.py:36
  130.7 2.4 %fusion.1 = f32[128,512]{1,0:T(8,128)} fusion(f32[128,512]{1,0:T(8,128)} %reduce-scatter.2.cloned.1.call-done, f32[4,128,128]{1,2,0:T(8,128)S(1)} %bitcast_multiply_fusion, f32[4,128,512]{2,1,0:T(8,128)S(1)} %bitcast.51), kind=kOutput, calls=%fused_computation.6 | convolution fusion | flops 402718720 | bytes 1835008 | tf_op jit(solution)/shard_map/dab,dbp->ap/dot_general | solution.py:32
  133.1 0.0 all-to-all-done
  133.1 48.7 %all-gather.5.cloned.1.call-done = f32[1024,512]{1,0:T(8,128)} async-done(((f32[128,512]{1,0:T(8,128)}), f32[1024,512]{1,0:T(8,128)}) %all-gather.5.cloned.1.call-update) | async-done | bytes 2097168 | tf_op jit(solution)/shard_map/all_gather | solution.py:20
  181.8 0.0 copy-start.1
  181.8 0.0 copy-start.2
  181.8 3.4 %convolution_bitcast_fusion = f32[128,512]{1,0:T(8,128)S(1)} fusion(f32[8,128,512]{2,1,0:T(8,128)} %bitcast.53, f32[8,128,128]{1,2,0:T(8,128)} %all-to-all-done, f32[8]{0:T(128)S(1)} %compare_convert_fusion.1, f32[1,8,128,128]{3,2,1,0:T(8,128)} %param.9), kind=kOutput, calls=%fused_computation.1 | convolution fusion | flops 805568512 | bytes 3407904 | tf_op jit(solution)/shard_map/jab,jbp->ap/dot_general | solution.py:25
  185.2 1.3 fusion
  186.5 0.0 copy-done.1
  186.6 0.0 copy-done.2
  186.6 4.4 %bitcast_add_fusion = f32[1024,512]{1,0:T(8,128)} fusion(f32[1024,512]{1,0:T(8,128)S(1)} %copy-done.2, f32[1024,512]{1,0:T(8,128)S(1)} %copy-done.1, f32[128,512]{1,0:T(8,128)S(1)} %fusion, f32[1024,128]{1,0:T(8,128)} %param.8), kind=kOutput, calls=%fused_computation | convolution fusion | flops 806354944 | bytes 7077888 | tf_op jit(solution)/shard_map/dot_general | solution.py:43
  (2 shorter events, 0.0 us)
Async XLA Ops:
  6.5 1.6 copy-start
  6.5 4.0 %copy-start.6 = (f32[1,128,128]{2,1,0:T(8,128)S(1)}, f32[1,128,128]{2,1,0:T(8,128)}, u32[]{:S(2)}) copy-start(f32[1,128,128]{2,1,0:T(8,128)} %param.10) | copy-start | bytes 196612
  6.5 79.3 %copy-start.5 = (f32[1,4,128,128]{3,2,1,0:T(8,128)S(1)}, f32[1,4,128,128]{3,2,1,0:T(8,128)}, u32[]{:S(2)}) copy-start(f32[1,4,128,128]{3,2,1,0:T(8,128)} %param.11) | copy-start | bytes 786436
  6.5 79.2 %all-reduce.2.cloned.1.call-start = ((), (), s32[]{:S(2)}) async-start(), calls=%async_computation.2 | async-start | bytes 524288 | tf_op jit(solution)/shard_map/psum | solution.py:30
  10.5 78.5 %copy-start.3 = (f32[128,512]{1,0:T(8,128)}, f32[128,512]{1,0:T(8,128)S(1)}, u32[]{:S(2)}) copy-start(f32[128,512]{1,0:T(8,128)S(1)} %fusion.10) | copy-start | bytes 786436
  11.9 102.3 %all-gather.7.cloned.1.call-start = ((), (), s32[]{:S(2)}) async-start(), calls=%async_computation.5 | async-start | bytes 1310720 | tf_op jit(solution)/shard_map/all_gather | solution.py:31
  85.8 3.9 %copy-start.4 = (f32[1,8,128,128]{3,2,1,0:T(8,128)S(1)}, f32[1,8,128,128]{3,2,1,0:T(8,128)}, u32[]{:S(2)}) copy-start(f32[1,8,128,128]{3,2,1,0:T(8,128)} %param.9) | copy-start | bytes 1572868
  85.8 44.9 %reduce-scatter.2.cloned.1.call-start = ((), (), s32[]{:S(2)}) async-start(), calls=%async_computation.3 | async-start | bytes 1310720 | tf_op jit(solution)/shard_map/reduce_scatter | solution.py:36
  89.1 92.8 %all-gather.5.cloned.1.call-start = ((), (), s32[]{:S(2)}) async-start(), calls=%async_computation.4 | async-start | bytes 2359296 | tf_op jit(solution)/shard_map/all_gather | solution.py:20
  90.6 42.5 %all-to-all-start = ((f32[8,128,128]{1,2,0:T(8,128)}), f32[8,128,128]{1,2,0:T(8,128)}, u32[]{:S(2)}, u32[]{:S(2)}) async-start(f32[8,128,128]{1,2,0:T(8,128)} %copy.9), calls=%async_computation | async-start | bytes 1048576 | tf_op jit(solution)/shard_map/all_to_all | solution.py:18
  181.8 4.7 %copy-start.1 = (f32[1024,512]{1,0:T(8,128)S(1)}, f32[1024,512]{1,0:T(8,128)}, u32[]{:S(2)}) copy-start(f32[1024,512]{1,0:T(8,128)} %fusion.9) | copy-start | bytes 6291460
  181.8 4.7 %copy-start.2 = (f32[1024,512]{1,0:T(8,128)S(1)}, f32[1024,512]{1,0:T(8,128)}, u32[]{:S(2)}) copy-start(f32[1024,512]{1,0:T(8,128)} %fusion.8) | copy-start | bytes 6291460
Sparse Core Ops, SparseCore 0:
  12.0 73.7 all-reduce.1
  87.3 16.0 all-gather.6
  105.9 24.7 reduce-scatter.1
  132.7 49.0 all-gather.4
where the time goes:
time: 198 us; the launch traced here: 197 us
  waiting for transfers between devices  138 us (70%)
  matrix products  37.3 us (19%)
  between operations  13.3 us (7%)
  starting transfers between devices  4.44 us (2%)
  local copies, waits for them, and re-layouts  4.31 us (2%)
    psum x1, waiting for transfers between devices, local(): g_whole = lax.psum(local_g, 'leaf')  73.8 us
    all_gather x1, waiting for transfers between devices, local(): piece = lax.all_gather(coef[None], 'leaf', axis=0, tiled=True)  48.7 us
    reduce_scatter x1, waiting for transfers between devices, local(): lax.psum_scatter(terms.reshape(number * rank_two, g_whole.shape[1]), 'clu...  15 us
    dot_general x1, matrix products, local(): jnp.dot(dense_leaf.T, probes, precision=HI)  9.6 us
    dot_general x1, matrix products, local(): jnp.dot(dense_leaf, probes, precision=HI)  9.59 us
    dot_general x1, matrix products, local(): return near + jnp.dot(leaf_basis, total, precision=HI)  4.38 us
    all_to_all x1, starting transfers between devices, local(): lax.all_to_all(cores, 'leaf', split_axis=0, concat_axis=0, tiled=True)  4.32 us
  transfers between devices with their start and end apart: 5, of which 3 were waited for; matrix products, arithmetic and copies ran while one was open for 14% of the time, Pallas kernels for 0%

commit v1 on v0

--- a/solution.py
+++ b/solution.py
@@ -17,7 +17,9 @@
     coef = jnp.dot(leaf_basis.T, probes, precision=HI)
     turned = lax.all_to_all(cores, "leaf", split_axis=0, concat_axis=0, tiled=True)
     used = cores + jnp.transpose(turned, (0, 2, 1))
-    piece = lax.all_gather(coef[None], "leaf", axis=0, tiled=True)
+    x = coef[None]
+    sent = jnp.stack([x] * lax.axis_size("leaf"))
+    piece = jnp.concatenate(lax.all_to_all(sent, "leaf", 0, 0), axis=0)
     count = piece.shape[0]
     block = used
     keep = (jnp.arange(count, dtype=jnp.int32) != own).astype(jnp.float32)

time: 198 us -> 162 us (0.82)
  waiting for transfers between devices: 138 us -> 96.7 us
  starting transfers between devices: 4.44 us -> 12 us
  matrix products: 37.3 us -> 34.1 us
    all_gather x1 -> x0, waiting for transfers between devices: 48.7 us -> none  [local(): piece = lax.all_gather(coef[None], 'leaf', axis=0, tiled=True)]
    all_to_all x0 -> x1, waiting for transfers between devices: none -> 5.45 us  [local(): piece = jnp.concatenate(lax.all_to_all(sent, 'leaf', 0, 0), axis=0)]
    all_to_all x0 -> x1, starting transfers between devices: none -> 4.47 us  [local(): piece = jnp.concatenate(lax.all_to_all(sent, 'leaf', 0, 0), axis=0)]
    all_to_all x1, starting transfers between devices: 4.32 us -> 7.44 us  [local(): lax.all_to_all(cores, 'leaf', split_axis=0, concat_axis=0, tiled=True)]
  transfers between devices with their start and end apart: 5 -> 5, of which waited for: 3 -> 3; matrix products, arithmetic and copies ran while one was open for 14% -> 18% of each run, Pallas kernels for 0% -> 0%
where the time goes in v1:
time: 162 us
  waiting for transfers between devices  96.7 us (60%)
  matrix products  34.1 us (21%)
  between operations  13.3 us (8%)
  starting transfers between devices  12 us (7%)
  local copies, waits for them, and re-layouts  5.6 us (3%)
    psum x1, waiting for transfers between devices, local(): g_whole = lax.psum(local_g, 'leaf')  74.3 us
    reduce_scatter x1, waiting for transfers between devices, local(): lax.psum_scatter(terms.reshape(number * rank_two, g_whole.shape[1]), 'clu...  16.9 us
    dot_general x1, matrix products, local(): jnp.dot(dense_leaf, probes, precision=HI)  9.76 us
    dot_general x1, matrix products, local(): jnp.dot(dense_leaf.T, probes, precision=HI)  8.12 us
    all_to_all x1, starting transfers between devices, local(): lax.all_to_all(cores, 'leaf', split_axis=0, concat_axis=0, tiled=True)  7.44 us
    all_to_all x1, waiting for transfers between devices, local(): piece = jnp.concatenate(lax.all_to_all(sent, 'leaf', 0, 0), axis=0)  5.45 us
    all_to_all x1, starting transfers between devices, local(): piece = jnp.concatenate(lax.all_to_all(sent, 'leaf', 0, 0), axis=0)  4.47 us
    dot_general x1, matrix products, local(): return near + jnp.dot(leaf_basis, total, precision=HI)  4.38 us
  transfers between devices with their start and end apart: 5, of which 3 were waited for; matrix products, arithmetic and copies ran while one was open for 18% of the time, Pallas kernels for 0%

profile of v1, /device:TPU:0, one launch (start us, length us, event | category | flops | bytes accessed | tf_op | source)
XLA Modules:
  0.0 161.8 jit_solution(14283489218369075645)
XLA Ops:
  6.5 0.0 copy-start
  6.5 0.0 copy-start.4
  6.5 2.2 %copy.9 = f32[8,128,128]{1,2,0:T(8,128)} copy(f32[8,128,128]{2,1,0:T(8,128)} %bitcast.56) | data formatting | bytes 1048576 | tf_op jit(solution)/shard_map/squeeze | solution.py:12
  8.7 0.0 copy-start.8
  8.7 7.4 %all-to-all-start = ((f32[8,128,128]{1,2,0:T(8,128)}), f32[8,128,128]{1,2,0:T(8,128)S(1)}, u32[]{:S(2)}, u32[]{:S(2)}) async-start(f32[8,128,128]{1,2,0:T(8,128)} %copy.9), calls=%async_computation | async-start | bytes 1048576 | tf_op jit(solution)/shard_map/all_to_all | solution.py:18
  16.2 0.0 all-reduce.2.cloned.1.call-start
  16.2 0.0 copy-done
  16.2 0.0 copy-done.4
  16.2 1.4 fusion.15
  17.6 0.0 copy-done.8
  17.6 1.3 convolution_bitcast_fusion.2
  18.9 0.0 all-reduce.2.cloned.1.call-update
  18.9 0.0 all-gather.3.cloned.1.call-start
  19.0 74.3 %all-reduce.2.cloned.1.call-done = f32[128,512]{0,1:T(8,128)} async-done(((f32[128,512]{0,1:T(8,128)}), f32[128,512]{0,1:T(8,128)}) %all-reduce.2.cloned.1.call-update) | async-done | bytes 262160 | tf_op jit(solution)/shard_map/psum | solution.py:32
  93.3 0.0 all-gather.3.cloned.1.call-update
  93.3 0.0 all-to-all-done
  93.3 0.0 copy-start.5
  93.3 1.6 %stack.3 = f32[8,1,128,512]{3,2,1,0:T(8,128)} broadcast(f32[128,512]{1,0:T(8,128)S(1)} %fusion.15), dimensions={2,3} | broadcast | bytes 2359296 | tf_op jit(solution)/shard_map/stack | solution.py:21
  94.9 0.0 copy-start.7
  94.9 0.0 copy-start.6
  94.9 0.0 copy-done.5
  94.9 4.5 %all-to-all-start.1 = ((f32[8,1,128,512]{3,2,1,0:T(8,128)}), f32[8,1,128,512]{3,2,1,0:T(8,128)}, u32[]{:S(2)}, u32[]{:S(2)}) async-start(f32[8,1,128,512]{3,2,1,0:T(8,128)} %stack.3), calls=%async_computation.1 | async-start | bytes 4194304 | tf_op jit(solution)/shard_map/all_to_all | solution.py:22
  99.4 0.0 reduce-scatter.2.cloned.1.call-start
  99.5 0.0 copy-done.7
  99.5 0.1 copy.10
  99.6 0.1 bitcast_multiply_fusion
  99.7 0.0 copy-done.6
  99.7 2.0 %fusion.16 = f32[512,512]{1,0:T(8,128)} fusion(f32[512,128]{1,0:T(8,128)S(1)} %bitcast.55, f32[128,512]{0,1:T(8,128)S(1)} %copy-done.6), kind=kOutput, calls=%fused_computation.21 | convolution fusion | flops 402653184 | bytes 1572864 | tf_op jit(solution)/shard_map/dba,bp->dap/dot_general | solution.py:37
  101.8 0.0 reduce-scatter.2.cloned.1.call-update
  101.8 0.0 copy-start.1
  101.8 9.8 %fusion.13 = f32[1024,512]{1,0:T(8,128)} fusion(f32[1024,1024]{1,0:T(8,128)} %param.7, f32[1024,512]{1,0:T(8,128)S(1)} %copy-done), kind=kOutput, calls=%fused_computation.18 | convolution fusion | flops 6442450944 | bytes 8388608 | tf_op jit(solution)/shard_map/dot_general | solution.py:16
  111.6 0.0 copy-done.1
  111.6 8.1 %fusion.14 = f32[1024,512]{1,0:T(8,128)} fusion(f32[1024,1024]{1,0:T(8,128)S(1)} %copy-done.1, f32[1024,512]{1,0:T(8,128)S(1)} %copy-done), kind=kOutput, calls=%fused_computation.19 | convolution fusion | flops 6442450944 | bytes 8388608 | tf_op jit(solution)/shard_map/dot_general | solution.py:16
  119.7 0.0 all-gather.3.cloned.1.call-done
  119.7 1.6 %copy.14 = f32[512,512]{1,0:T(8,128)S(1)} copy(f32[512,512]{0,1:T(8,128)} %all-gather.3.cloned.1.call-done) | data formatting | bytes 2097152 | tf_op jit(solution)/shard_map/all_gather | solution.py:33
  121.4 16.9 %reduce-scatter.2.cloned.1.call-done = f32[128,512]{1,0:T(8,128)} async-done(((f32[512,512]{1,0:T(8,128)}), f32[128,512]{1,0:T(8,128)}) %reduce-scatter.2.cloned.1.call-update) | async-done | bytes 262160 | tf_op jit(solution)/shard_map/reduce_scatter | solution.py:38
  138.2 2.4 %fusion.6 = f32[128,512]{1,0:T(8,128)} fusion(f32[128,512]{1,0:T(8,128)} %reduce-scatter.2.cloned.1.call-done, f32[4,128,128]{1,2,0:T(8,128)S(1)} %bitcast_multiply_fusion, f32[4,128,512]{2,1,0:T(8,128)S(1)} %bitcast.54), kind=kOutput, calls=%fused_computation.8 | convolution fusion | flops 402718720 | bytes 1835008 | tf_op jit(solution)/shard_map/dab,dbp->ap/dot_general | solution.py:34
  140.7 5.5 %all-to-all-done.1 = f32[8,1,128,512]{3,2,1,0:T(8,128)} async-done(((f32[8,1,128,512]{3,2,1,0:T(8,128)}), f32[8,1,128,512]{3,2,1,0:T(8,128)}, u32[]{:S(2)}, u32[]{:S(2)}) %all-to-all-start.1) | async-done | bytes 2097184 | tf_op jit(solution)/shard_map/all_to_all | solution.py:22
  146.1 0.0 copy-start.2
  146.1 0.0 copy-start.3
  146.1 3.4 %fusion.2 = f32[128,512]{1,0:T(8,128)S(1)} fusion(f32[8,1,128,512]{3,2,1,0:T(8,128)} %all-to-all-done.1, f32[8,128,128]{1,2,0:T(8,128)} %copy-done.5, f32[8]{0:T(128)S(1)} %compare_convert_fusion.1, f32[1,8,128,128]{3,2,1,0:T(8,128)} %param.9), kind=kOutput, calls=%fused_computation.3 | convolution fusion | flops 805568512 | bytes 3407904 | tf_op jit(solution)/shard_map/jab,jbp->ap/dot_general | solution.py:27
  149.5 1.3 fusion.5
  150.8 0.0 copy-done.2
  150.9 0.0 copy-done.3
  150.9 4.4 %bitcast_add_fusion = f32[1024,512]{1,0:T(8,128)} fusion(f32[1024,512]{1,0:T(8,128)S(1)} %copy-done.3, f32[1024,512]{1,0:T(8,128)S(1)} %copy-done.2, f32[128,512]{1,0:T(8,128)S(1)} %fusion.5, f32[1024,128]{1,0:T(8,128)} %param.8), kind=kOutput, calls=%fused_computation | convolution fusion | flops 806354944 | bytes 7077888 | tf_op jit(solution)/shard_map/dot_general | solution.py:45
  (2 shorter events, 0.0 us)
Async XLA Ops:
  6.5 9.7 %copy-start = (f32[1024,512]{1,0:T(8,128)S(1)}, f32[1024,512]{1,0:T(8,128)}, u32[]{:S(2)}) copy-start(f32[1024,512]{1,0:T(8,128)} %param.6) | copy-start | bytes 6291460
  6.5 9.7 %copy-start.4 = (f32[1024,128]{1,0:T(8,128)S(1)}, f32[1024,128]{1,0:T(8,128)}, u32[]{:S(2)}) copy-start(f32[1024,128]{1,0:T(8,128)} %param.8) | copy-start | bytes 1572868
  8.7 8.9 %copy-start.8 = (f32[1,128,128]{2,1,0:T(8,128)S(1)}, f32[1,128,128]{2,1,0:T(8,128)}, u32[]{:S(2)}) copy-start(f32[1,128,128]{2,1,0:T(8,128)} %param.10) | copy-start | bytes 196612
  8.7 84.6 %all-to-all-start = ((f32[8,128,128]{1,2,0:T(8,128)}), f32[8,128,128]{1,2,0:T(8,128)S(1)}, u32[]{:S(2)}, u32[]{:S(2)}) async-start(f32[8,128,128]{1,2,0:T(8,128)} %copy.9), calls=%async_computation | async-start | bytes 1048576 | tf_op jit(solution)/shard_map/all_to_all | solution.py:18
  16.2 77.1 %all-reduce.2.cloned.1.call-start = ((), (), s32[]{:S(2)}) async-start(), calls=%async_computation.3 | async-start | bytes 524288 | tf_op jit(solution)/shard_map/psum | solution.py:32
  18.9 100.8 %all-gather.3.cloned.1.call-start = ((), (), s32[]{:S(2)}) async-start(), calls=%async_computation.5 | async-start | bytes 1310720 | tf_op jit(solution)/shard_map/all_gather | solution.py:33
  93.3 1.6 %copy-start.5 = (f32[8,128,128]{1,2,0:T(8,128)}, f32[8,128,128]{1,2,0:T(8,128)S(1)}, u32[]{:S(2)}) copy-start(f32[8,128,128]{1,2,0:T(8,128)S(1)} %all-to-all-done) | copy-start | bytes 1572868
  94.9 4.5 %copy-start.7 = (f32[1,4,128,128]{3,2,1,0:T(8,128)S(1)}, f32[1,4,128,128]{3,2,1,0:T(8,128)}, u32[]{:S(2)}) copy-start(f32[1,4,128,128]{3,2,1,0:T(8,128)} %param.11) | copy-start | bytes 786436
  94.9 4.8 %copy-start.6 = (f32[128,512]{0,1:T(8,128)S(1)}, f32[128,512]{0,1:T(8,128)}, u32[]{:S(2)}) copy-start(f32[128,512]{0,1:T(8,128)} %all-reduce.2.cloned.1.call-done) | copy-start | bytes 786436
  94.9 51.2 %all-to-all-start.1 = ((f32[8,1,128,512]{3,2,1,0:T(8,128)}), f32[8,1,128,512]{3,2,1,0:T(8,128)}, u32[]{:S(2)}, u32[]{:S(2)}) async-start(f32[8,1,128,512]{3,2,1,0:T(8,128)} %stack.3), calls=%async_computation.1 | async-start | bytes 4194304 | tf_op jit(solution)/shard_map/all_to_all | solution.py:22
  99.4 38.8 %reduce-scatter.2.cloned.1.call-start = ((), (), s32[]{:S(2)}) async-start(), calls=%async_computation.4 | async-start | bytes 1310720 | tf_op jit(solution)/shard_map/reduce_scatter | solution.py:38
  101.8 9.8 %copy-start.1 = (f32[1024,1024]{1,0:T(8,128)S(1)}, f32[1024,1024]{1,0:T(8,128)}, u32[]{:S(2)}) copy-start(f32[1024,1024]{1,0:T(8,128)} %param.7) | copy-start | bytes 12582916
  146.1 4.7 %copy-start.2 = (f32[1024,512]{1,0:T(8,128)S(1)}, f32[1024,512]{1,0:T(8,128)}, u32[]{:S(2)}) copy-start(f32[1024,512]{1,0:T(8,128)} %fusion.14) | copy-start | bytes 6291460
  146.1 4.7 %copy-start.3 = (f32[1024,512]{1,0:T(8,128)S(1)}, f32[1024,512]{1,0:T(8,128)}, u32[]{:S(2)}) copy-start(f32[1024,512]{1,0:T(8,128)} %fusion.13) | copy-start | bytes 6291460
Sparse Core Ops, SparseCore 0:
  20.3 72.9 all-reduce.1
  94.8 16.0 all-gather.2
  113.4 24.7 reduce-scatter.1
